TPU v7x, 128 devices: a whole 4x4x4 slice. The times are simulated.
128 devices in a mesh: row: 16 (over y, z), col: 8 (over x, core).
Axes of the slice: x: 4, y: 4, z: 4, core: 2. Of those that a mesh axis runs over, the one named last changes fastest.
Arguments:
- queries: bfloat16 [49152, 4096], P(('row', 'col')), may hold values from -6 to 6
- keys: bfloat16 [65536, 256], P(('row', 'col')), may hold values from -6 to 6
- values: bfloat16 [65536, 256], P(('row', 'col')), may hold values from -6 to 6
- output_gradient: bfloat16 [49152, 4096], P(('row', 'col')), may hold values from -6 to 6
- tile_block_table: int32 [384, 3], P(('row', 'col')), may hold values from 0 to 127, as said below
Outputs:
- dqueries: bfloat16 [49152, 4096], P(('row', 'col'))
- dkeys: bfloat16 [65536, 256], P(('row', 'col'))
- dvalues: bfloat16 [65536, 256], P(('row', 'col'))
Inputs may be any that keep to these rules, and one draw needn't show every extreme that they name: `tile_block_table`: A tile's first id is the block that holds its own query rows; its 3 ids are distinct and none is larger than that block. Block b is held by the device of index b // 1 in the order row-major over (row, col). The tiles of one device name at most 1 distinct blocks held on devices of one col index, and at most 2 distinct blocks held on devices of one row index.
All inputs are finite; a program needn't handle non-finite values.
Results may differ from a plain program's by a relative error of at most 0.0064.
Values may be sent and summed in bfloat16 or wider, within the bound.
A program may use at most 192 MiB of HBM per device.

v0:
```python
import jax
import jax.numpy as jnp
from jax import lax
from jax.sharding import PartitionSpec as P

QUERY_HEADS = 32
KEY_VALUE_HEADS = 2
HEAD_WIDTH = 128
GROUP_WIDTH = 16
TILE_QUERY_ROWS = 128
BLOCK_KEY_ROWS = 512
PICKED_BLOCKS = 3


def sent_to_all(value, axis):
    copies = jnp.broadcast_to(value, (lax.axis_size(axis), *value.shape))
    return lax.all_to_all(copies, axis, split_axis=0, concat_axis=0, tiled=True)


def joined_along(blocks, dim):
    shape = list(blocks.shape[1:])
    shape[dim] *= blocks.shape[0]
    return jnp.moveaxis(blocks, 0, dim).reshape(shape)


def gather_directly(value, axis, dim):
    blocks = sent_to_all(value, axis)
    return joined_along(blocks, dim)


def pair_grads(
    tile_query_rows, gradient_rows, block_key_rows, block_value_rows, query_place, key_place
):
    factor = HEAD_WIDTH ** (-0.5)
    forward = (((1,), (1,)), ((), ()))
    backward = (((0,), (0,)), ((), ()))
    scores = (
        lax.dot_general(
            tile_query_rows, block_key_rows, forward, preferred_element_type=jnp.float32
        )
        * factor
    )
    scores = jnp.where(key_place[None, :] <= query_place[:, None], scores, -jnp.inf)
    weights = jax.nn.softmax(scores, axis=-1)
    grad_weights = lax.dot_general(
        gradient_rows, block_value_rows, forward, preferred_element_type=jnp.float32
    )
    row_delta = jnp.sum(weights * grad_weights, axis=-1, keepdims=True)
    grad_scores = (weights * (grad_weights - row_delta) * factor).astype(jnp.bfloat16)
    query_gradient = jnp.dot(grad_scores, block_key_rows, preferred_element_type=jnp.float32)
    key_gradient = lax.dot_general(
        grad_scores, tile_query_rows, backward, preferred_element_type=jnp.float32
    )
    value_gradient = lax.dot_general(
        weights.astype(jnp.bfloat16), gradient_rows, backward, preferred_element_type=jnp.float32
    )
    return (query_gradient, key_gradient, value_gradient)


def item_grads(packed):
    query_item, gradient_item, block_item, query_place, key_place = packed
    return pair_grads(
        query_item, gradient_item, block_item[0], block_item[1], query_place, key_place
    )


def local(queries, keys, values, output_gradient, tile_block_table):
    n_row = lax.axis_size("row")
    n_col = lax.axis_size("col")
    my_row = lax.axis_index("row")
    my_col = lax.axis_index("col")
    devices = n_row * n_col
    my_device = my_row * n_col + my_col
    blk_dev = keys.shape[0] // BLOCK_KEY_ROWS
    device_tile_count = tile_block_table.shape[0]
    kv_width = keys.shape[1]
    cap_row = 2 * blk_dev
    nblocks = devices * blk_dev
    band_rows = n_row * blk_dev
    flat_width = BLOCK_KEY_ROWS * 2 * kv_width
    starting_position = nblocks * BLOCK_KEY_ROWS - devices * device_tile_count * TILE_QUERY_ROWS
    catalog = jnp.arange(nblocks, dtype=jnp.int32)
    row_lists = gather_directly(tile_block_table, "col", 0)
    wanted = jnp.any(
        row_lists.reshape(n_col, device_tile_count * PICKED_BLOCKS, 1) == catalog, axis=1
    ).astype(jnp.int32)
    layout = wanted.reshape(n_col, n_row, n_col, blk_dev)
    by_col = jnp.transpose(layout, (0, 2, 1, 3)).reshape(n_col, n_col, band_rows)
    col_rank = jnp.cumsum(by_col, axis=2) - by_col
    local_kv = jnp.concatenate((keys, values), axis=1)
    column = lax.all_gather(local_kv, "row", axis=0, tiled=True).reshape(band_rows, flat_width)
    row_wants = by_col[:, my_col, :]
    row_ranks = col_rank[:, my_col, :]
    slot_ids = jnp.arange(blk_dev, dtype=jnp.int32)
    picker = (row_ranks[:, None, :] == slot_ids[None, :, None]) & (row_wants[:, None, :] == 1)
    picker = picker.astype(jnp.bfloat16).reshape(n_col * blk_dev, band_rows)
    outgoing = jnp.dot(picker, column, preferred_element_type=jnp.float32).astype(jnp.bfloat16)
    landed_parts = lax.all_to_all(
        outgoing.reshape(n_col, blk_dev, flat_width), "col", split_axis=0, concat_axis=0, tiled=True
    )
    landed_parts = landed_parts.reshape(n_col * blk_dev, BLOCK_KEY_ROWS, 2 * kv_width)
    my_lists = tile_block_table.reshape(device_tile_count * PICKED_BLOCKS)
    holder = my_lists // blk_dev
    holder_row = holder // n_col
    holder_col = holder % n_col
    within = my_lists % blk_dev
    my_ranks = col_rank[my_col]
    paired_position = holder_col * blk_dev + my_ranks[holder_col, holder_row * blk_dev + within]
    paired_key_value = jnp.take(landed_parts, paired_position, axis=0).reshape(
        device_tile_count, PICKED_BLOCKS * BLOCK_KEY_ROWS, 2, KEY_VALUE_HEADS, HEAD_WIDTH
    )
    entry_count = device_tile_count * KEY_VALUE_HEADS
    tile_query_rows = queries.reshape(
        device_tile_count, TILE_QUERY_ROWS, KEY_VALUE_HEADS, GROUP_WIDTH, HEAD_WIDTH
    ).transpose(0, 2, 3, 1, 4)
    tile_query_rows = tile_query_rows.reshape(
        entry_count, GROUP_WIDTH * TILE_QUERY_ROWS, HEAD_WIDTH
    )
    gradient_rows = output_gradient.reshape(
        device_tile_count, TILE_QUERY_ROWS, KEY_VALUE_HEADS, GROUP_WIDTH, HEAD_WIDTH
    ).transpose(0, 2, 3, 1, 4)
    gradient_rows = gradient_rows.reshape(entry_count, GROUP_WIDTH * TILE_QUERY_ROWS, HEAD_WIDTH)
    block_rows = paired_key_value.transpose(0, 3, 2, 1, 4).reshape(
        entry_count, 2, PICKED_BLOCKS * BLOCK_KEY_ROWS, HEAD_WIDTH
    )
    global_tile_index = my_device * device_tile_count + jnp.arange(
        device_tile_count, dtype=jnp.int32
    )
    rows_per_head = jnp.arange(GROUP_WIDTH * TILE_QUERY_ROWS, dtype=jnp.int32) % TILE_QUERY_ROWS
    query_place = jnp.repeat(
        starting_position + global_tile_index[:, None] * TILE_QUERY_ROWS + rows_per_head[None, :],
        KEY_VALUE_HEADS,
        axis=0,
    )
    row_offsets = jnp.arange(BLOCK_KEY_ROWS, dtype=jnp.int32)
    key_place = jnp.repeat(
        (tile_block_table[:, :, None] * BLOCK_KEY_ROWS + row_offsets).reshape(
            device_tile_count, PICKED_BLOCKS * BLOCK_KEY_ROWS
        ),
        KEY_VALUE_HEADS,
        axis=0,
    )
    query_gradient, key_gradient, value_gradient = lax.map(
        item_grads, (tile_query_rows, gradient_rows, block_rows, query_place, key_place)
    )
    dqueries = query_gradient.reshape(
        device_tile_count, KEY_VALUE_HEADS, GROUP_WIDTH, TILE_QUERY_ROWS, HEAD_WIDTH
    ).transpose(0, 3, 1, 2, 4)
    dqueries = dqueries.reshape(
        device_tile_count * TILE_QUERY_ROWS, QUERY_HEADS * HEAD_WIDTH
    ).astype(jnp.bfloat16)
    paired_terms = jnp.stack((key_gradient, value_gradient), axis=0).reshape(
        2, device_tile_count, KEY_VALUE_HEADS, PICKED_BLOCKS, BLOCK_KEY_ROWS, HEAD_WIDTH
    )
    paired_terms = paired_terms.transpose(1, 3, 4, 0, 2, 5).reshape(
        device_tile_count * PICKED_BLOCKS, flat_width
    )
    row_span = n_col * blk_dev
    col_lists = gather_directly(tile_block_table, "row", 0)
    col_wanted = jnp.any(
        col_lists.reshape(n_row, device_tile_count * PICKED_BLOCKS, 1) == catalog, axis=1
    ).astype(jnp.int32)
    by_row = col_wanted.reshape(n_row, n_row, row_span)
    row_rank = jnp.cumsum(by_row, axis=2) - by_row
    own_ranks = row_rank[my_row]
    row_slot = holder_row * cap_row + own_ranks[holder_row, holder_col * blk_dev + within]
    slot_count = n_row * cap_row
    assign = (row_slot[None, :] == jnp.arange(slot_count, dtype=jnp.int32)[:, None]).astype(
        jnp.float32
    )
    partials = jnp.dot(
        assign, paired_terms, precision=lax.Precision.HIGHEST, preferred_element_type=jnp.float32
    ).astype(jnp.bfloat16)
    returned = lax.all_to_all(
        partials.reshape(n_row, cap_row, flat_width), "row", split_axis=0, concat_axis=0, tiled=True
    )
    returned = returned.reshape(slot_count, flat_width)
    sender_wants = by_row[:, my_row, :]
    sender_ranks = row_rank[:, my_row, :]
    row_slot_ids = jnp.arange(cap_row, dtype=jnp.int32)
    collect = (sender_ranks[:, None, :] == row_slot_ids[None, :, None]) & (
        sender_wants[:, None, :] == 1
    )
    collect = collect.astype(jnp.bfloat16).reshape(slot_count, row_span).T
    result = lax.psum_scatter(
        jnp.dot(collect, returned, preferred_element_type=jnp.float32),
        "col",
        scatter_dimension=0,
        tiled=True,
    )
    result = result.reshape(blk_dev * BLOCK_KEY_ROWS, 2 * kv_width)
    return (
        dqueries,
        result[:, :kv_width].astype(jnp.bfloat16),
        result[:, kv_width:].astype(jnp.bfloat16),
    )


def solution(mesh):
    return jax.shard_map(
        local,
        mesh=mesh,
        in_specs=(
            P(("row", "col"), None),
            P(("row", "col"), None),
            P(("row", "col"), None),
            P(("row", "col"), None),
            P(("row", "col"), None),
        ),
        out_specs=(P(("row", "col"), None), P(("row", "col"), None), P(("row", "col"), None)),
        check_vma=False,
    )
```

profile of v0, /device:TPU:87, one launch (start us, length us, event | category | flops | bytes accessed | tf_op | source)
XLA Modules:
  0.0 976.6 jit_solution(15433184357276598834)
XLA Ops:
  10.4 5.1 all-to-all-start
  19.7 6.8 all-to-all-start.2
  28.7 52.8 %all-gather.2.cloned.1.call-done = bf16[8192,512]{1,0:T(8,128)(2,1)} async-done(((bf16[512,512]{1,0:T(8,128)(2,1)}), bf16[8192,512]{1,0:T(8,128)(2,1)}) %all-gather.2.cloned.1.call-update) | async-done | bytes 8388624 | tf_op jit(solution)/shard_map/all_gather | solution.py:91
  81.5 8.0 reshape.350
  89.4 6.6 fusion.27
  96.5 6.3 reduce.7
  102.8 8.0 reshape.390
  110.8 6.3 all-to-all-start.1
  127.0 37.2 %all-to-all-done.1 = bf16[8,2,131072]{2,1,0:T(2,128)(2,1)} async-done(((bf16[8,2,131072]{2,1,0:T(2,128)(2,1)}), bf16[8,2,131072]{2,1,0:T(2,128)(2,1)}, u32[]{:S(2)}, u32[]{:S(2)}) %all-to-all-start.1) | async-done | bytes 4194336 | tf_op jit(solution)/shard_map/all_to_all | solution.py:98
  164.1 8.8 reshape.391
  172.9 26.5 %reduce.2 = bf16[8,262144]{1,0:T(8,128)(2,1)} reduce(bf16[8,1,262144]{2,1,0:T(2,128)(2,1)} %reshape.391, bf16[]{:T(256)} %constant.181), dimensions={1}, to_apply=%all_to_all.13.reduce_sub_computation | reduce | bytes 8388610 | tf_op jit(solution)/shard_map/all_to_all | solution.py:98
  199.4 5.5 copy.115
  204.9 5.8 gather_fusion.1
  210.7 7.8 gather.20
  218.5 11.5 %fusion.29 = bf16[3,2,2,1536,128]{4,1,2,3,0:T(2,128)(2,1)S(1)} fusion(bf16[3,1536,2,2,128]{4,3,2,1,0:T(2,128)(2,1)} %gather.20, pred[3,1536]{1,0:T(4,128)(4,1)S(1)} %bitcast.152), kind=kLoop, calls=%fused_computation.42 | loop fusion | flops 2359296 | bytes 9441792 | tf_op jit(solution)/shard_map/transpose | solution.py:123
  232.9 227.2 %while.14 = (s32[]{:T(128)}, bf16[6,2048,128]{2,1,0:T(8,128)(2,1)}, f32[6,1536,128]{2,1,0:T(8,128)}, f32[6,1536,128]{2,1,0:T(8,128)}, s32[6,1536]{1,0:T(8,128)S(...) while((s32[]{:T(128)}, bf16[6,2048,128]{2,1,0:T(8,128)(2,1)}, ...), condition=%wide.region_6.7_spmd, body=%wide.region_2.6_spmd.sunk | while | flops 4086294528 | bytes 213654736 | solution.py:143
  244.1 10.5 %multiply_reduce_fusion.2 = (f32[2048]{0:T(1024)S(1)}, f32[2048,1536]{0,1:T(8,128)}) fusion(f32[2048]{0:T(1024)S(1)} %fusion.73, f32[2048,1536]{0,1:T(8,128)} %copy-done, f32[2048]{0:T(1024)S(1)} %get-tuple-element.142, bf16[6,2,1536,128]{3,2,1,0:T(8,128)(2,1)} %get-tuple-element.176, s32[]{:T(128)} %get-tuple-element.157, s32[]{:T(128)S(6)} %add.285, ...), kind=kOutput, calls=%fused_computation.4.clone.1 | convolution fusion | flops 817887232 | bytes 26108932 | tf_op jit(solution)/shard_map/while/body/eval_jaxpr/dot_general | solution.py:45
  256.8 6.7 multiply_convert_fusion.2
  263.4 3.8 fusion.75
  267.3 3.7 fusion.74
  282.0 10.5 %multiply_reduce_fusion.2 = (f32[2048]{0:T(1024)S(1)}, f32[2048,1536]{0,1:T(8,128)}) fusion(f32[2048]{0:T(1024)S(1)} %fusion.73, f32[2048,1536]{0,1:T(8,128)} %copy-done, f32[2048]{0:T(1024)S(1)} %get-tuple-element.142, bf16[6,2,1536,128]{3,2,1,0:T(8,128)(2,1)} %get-tuple-element.176, s32[]{:T(128)} %get-tuple-element.157, s32[]{:T(128)S(6)} %add.285, ...), kind=kOutput, calls=%fused_computation.4.clone.1 | convolution fusion | flops 817887232 | bytes 26108932 | tf_op jit(solution)/shard_map/while/body/eval_jaxpr/dot_general | solution.py:45
  294.6 6.7 multiply_convert_fusion.2
  301.3 3.8 fusion.75
  319.8 10.5 %multiply_reduce_fusion.2 = (f32[2048]{0:T(1024)S(1)}, f32[2048,1536]{0,1:T(8,128)}) fusion(f32[2048]{0:T(1024)S(1)} %fusion.73, f32[2048,1536]{0,1:T(8,128)} %copy-done, f32[2048]{0:T(1024)S(1)} %get-tuple-element.142, bf16[6,2,1536,128]{3,2,1,0:T(8,128)(2,1)} %get-tuple-element.176, s32[]{:T(128)} %get-tuple-element.157, s32[]{:T(128)S(6)} %add.285, ...), kind=kOutput, calls=%fused_computation.4.clone.1 | convolution fusion | flops 817887232 | bytes 26108932 | tf_op jit(solution)/shard_map/while/body/eval_jaxpr/dot_general | solution.py:45
  332.5 6.7 multiply_convert_fusion.2
  339.1 3.8 fusion.75
  357.6 10.5 %multiply_reduce_fusion.2 = (f32[2048]{0:T(1024)S(1)}, f32[2048,1536]{0,1:T(8,128)}) fusion(f32[2048]{0:T(1024)S(1)} %fusion.73, f32[2048,1536]{0,1:T(8,128)} %copy-done, f32[2048]{0:T(1024)S(1)} %get-tuple-element.142, bf16[6,2,1536,128]{3,2,1,0:T(8,128)(2,1)} %get-tuple-element.176, s32[]{:T(128)} %get-tuple-element.157, s32[]{:T(128)S(6)} %add.285, ...), kind=kOutput, calls=%fused_computation.4.clone.1 | convolution fusion | flops 817887232 | bytes 26108932 | tf_op jit(solution)/shard_map/while/body/eval_jaxpr/dot_general | solution.py:45
  370.2 6.7 multiply_convert_fusion.2
  376.9 3.8 fusion.75
  395.4 10.5 %multiply_reduce_fusion.2 = (f32[2048]{0:T(1024)S(1)}, f32[2048,1536]{0,1:T(8,128)}) fusion(f32[2048]{0:T(1024)S(1)} %fusion.73, f32[2048,1536]{0,1:T(8,128)} %copy-done, f32[2048]{0:T(1024)S(1)} %get-tuple-element.142, bf16[6,2,1536,128]{3,2,1,0:T(8,128)(2,1)} %get-tuple-element.176, s32[]{:T(128)} %get-tuple-element.157, s32[]{:T(128)S(6)} %add.285, ...), kind=kOutput, calls=%fused_computation.4.clone.1 | convolution fusion | flops 817887232 | bytes 26108932 | tf_op jit(solution)/shard_map/while/body/eval_jaxpr/dot_general | solution.py:45
  408.0 6.7 multiply_convert_fusion.2
  414.7 3.8 fusion.75
  433.2 10.5 %multiply_reduce_fusion.2 = (f32[2048]{0:T(1024)S(1)}, f32[2048,1536]{0,1:T(8,128)}) fusion(f32[2048]{0:T(1024)S(1)} %fusion.73, f32[2048,1536]{0,1:T(8,128)} %copy-done, f32[2048]{0:T(1024)S(1)} %get-tuple-element.142, bf16[6,2,1536,128]{3,2,1,0:T(8,128)(2,1)} %get-tuple-element.176, s32[]{:T(128)} %get-tuple-element.157, s32[]{:T(128)S(6)} %add.285, ...), kind=kOutput, calls=%fused_computation.4.clone.1 | convolution fusion | flops 817887232 | bytes 26108932 | tf_op jit(solution)/shard_map/while/body/eval_jaxpr/dot_general | solution.py:45
  445.8 6.7 multiply_convert_fusion.2
  452.5 3.8 fusion.75
  456.3 3.7 fusion.74
  460.1 6.0 copy.97
  466.1 6.0 copy.98
  472.1 5.5 maximum_bitcast_fusion
  477.6 22.3 %reshape.357 = f32[9,262144]{1,0:T(8,128)} reshape(f32[3,3,512,2,2,128]{5,4,3,2,1,0:T(2,128)} %maximum_bitcast_fusion) | data formatting | bytes 18874368 | tf_op jit(solution)/shard_map/reshape | solution.py:155
  499.9 23.0 %convolution_convert_fusion = bf16[32,262144]{1,0:T(8,128)(2,1)} fusion(f32[9,262144]{1,0:T(8,128)} %reshape.357, s32[9]{0:T(128)S(1)} %copy-done.7), kind=kOutput, calls=%fused_computation.35 | convolution fusion | flops 914358528 | bytes 26214436 | tf_op jit(solution)/shard_map/dot_general | solution.py:171
  523.0 16.2 %reshape.358 = bf16[16,2,262144]{2,1,0:T(2,128)(2,1)} reshape(bf16[32,262144]{1,0:T(8,128)(2,1)} %convolution_convert_fusion) | data formatting | bytes 33554432 | tf_op jit(solution)/shard_map/reshape | solution.py:175
  539.2 6.9 all-to-all-start.3
  548.1 3.9 copy.116
  555.3 288.0 %all-to-all-done.3 = bf16[16,2,262144]{2,1,0:T(2,128)(2,1)} async-done(((bf16[16,2,262144]{2,1,0:T(2,128)(2,1)}), bf16[16,2,262144]{2,1,0:T(2,128)(2,1)}, u32[]{:S(2)}, u32[]{:S(2)}) %all-to-all-start.3) | async-done | bytes 16777248 | tf_op jit(solution)/shard_map/all_to_all | solution.py:174
  843.3 18.1 %convolution_bitcast_fusion.2 = f32[8,262144]{1,0:T(8,128)} fusion(bf16[16,2,262144]{2,1,0:T(2,128)(2,1)} %all-to-all-done.3, s32[16,8]{0,1:T(8,128)S(1)} %dynamic-slice_bitcast_fusion.5, pred[16,8]{0,1:T(8,128)(4,1)S(1)} %fusion.41), kind=kOutput, calls=%fused_computation.36 | convolution fusion | flops 134218240 | bytes 25166464 | tf_op jit(solution)/shard_map/dot_general | solution.py:186
  861.5 94.9 %all-reduce.2 = bf16[8,262144]{1,0:T(8,128)(2,1)} all-reduce(f32[8,262144]{1,0:T(8,128)} %convolution_bitcast_fusion.2), channel_id=2, replica_groups=mesh['row'=16,'col'=8] {'col'}, use_global_device_ids=true, to_apply=%region_9.10.clone | all-reduce | flops 2097152 | bytes 12582912
  956.3 12.1 %fusion.30 = bf16[262144]{0:T(1024)(128)(2,1)S(1)} fusion(bf16[8,262144]{1,0:T(8,128)(2,1)} %all-reduce.2, u32[]{:T(128)} %bitcast.35), kind=kLoop, calls=%fused_computation.46 | loop fusion | bytes 1048580 | tf_op jit(solution)/shard_map/convert.3
  (140 shorter events, 123.0 us)
Async XLA Ops:
  7.2 74.3 %all-gather.2.cloned.1.call-start = ((), (), s32[]{:S(2)}) async-start(), calls=%async_computation.4 | async-start | bytes 8912896 | tf_op jit(solution)/shard_map/all_gather | solution.py:91
  10.4 8.0 all-to-all-start
  19.7 91.1 %all-to-all-start.2 = ((s32[16,3,3]{2,1,0:T(4,128)}), s32[16,3,3]{2,1,0:T(4,128)S(1)}, u32[]{:S(2)}, u32[]{:S(2)}) async-start(s32[16,3,3]{2,1,0:T(4,128)} %broadcast_in_dim.70), calls=%async_computation.2 | async-start | bytes 65536 | tf_op jit(solution)/shard_map/all_to_all | solution.py:17
  110.8 6.3 copy-start.6
  110.8 6.6 copy-start.2
  110.8 53.3 %all-to-all-start.1 = ((bf16[8,2,131072]{2,1,0:T(2,128)(2,1)}), bf16[8,2,131072]{2,1,0:T(2,128)(2,1)}, u32[]{:S(2)}, u32[]{:S(2)}) async-start(bf16[8,2,131072]{2,1,0:T(2,128)(2,1)} %reshape.390), calls=%async_computation.1 | async-start | bytes 8388608 | tf_op jit(solution)/shard_map/all_to_all | solution.py:98
  117.5 2.1 copy-start.3
  124.8 48.1 %copy-start.4 = (s32[16,128]{0,1:T(8,128)}, s32[16,128]{0,1:T(8,128)S(1)}, u32[]{:S(2)}) copy-start(s32[16,128]{0,1:T(8,128)S(1)} %copy.95) | copy-start | bytes 24580
  124.9 0.6 copy-start.5
  236.6 4.6 copy-start
  244.1 12.7 %copy-start.1 = (f32[2048,1536]{0,1:T(8,128)S(1)}, f32[2048,1536]{0,1:T(8,128)}, u32[]{:S(2)}) copy-start(f32[2048,1536]{0,1:T(8,128)} %copy-done) | copy-start | bytes 37748740 | tf_op jit(solution)/shard_map/while
  274.4 4.6 copy-start
  282.0 12.7 %copy-start.1 = (f32[2048,1536]{0,1:T(8,128)S(1)}, f32[2048,1536]{0,1:T(8,128)}, u32[]{:S(2)}) copy-start(f32[2048,1536]{0,1:T(8,128)} %copy-done) | copy-start | bytes 37748740 | tf_op jit(solution)/shard_map/while
  312.2 4.6 copy-start
  319.8 12.7 %copy-start.1 = (f32[2048,1536]{0,1:T(8,128)S(1)}, f32[2048,1536]{0,1:T(8,128)}, u32[]{:S(2)}) copy-start(f32[2048,1536]{0,1:T(8,128)} %copy-done) | copy-start | bytes 37748740 | tf_op jit(solution)/shard_map/while
  350.0 4.6 copy-start
  357.6 12.7 %copy-start.1 = (f32[2048,1536]{0,1:T(8,128)S(1)}, f32[2048,1536]{0,1:T(8,128)}, u32[]{:S(2)}) copy-start(f32[2048,1536]{0,1:T(8,128)} %copy-done) | copy-start | bytes 37748740 | tf_op jit(solution)/shard_map/while
  387.8 4.6 copy-start
  395.4 12.7 %copy-start.1 = (f32[2048,1536]{0,1:T(8,128)S(1)}, f32[2048,1536]{0,1:T(8,128)}, u32[]{:S(2)}) copy-start(f32[2048,1536]{0,1:T(8,128)} %copy-done) | copy-start | bytes 37748740 | tf_op jit(solution)/shard_map/while
  425.6 4.6 copy-start
  433.2 12.7 %copy-start.1 = (f32[2048,1536]{0,1:T(8,128)S(1)}, f32[2048,1536]{0,1:T(8,128)}, u32[]{:S(2)}) copy-start(f32[2048,1536]{0,1:T(8,128)} %copy-done) | copy-start | bytes 37748740 | tf_op jit(solution)/shard_map/while
  477.6 22.3 %copy-start.7 = (s32[9]{0:T(128)S(1)}, s32[9]{0:T(128)}, u32[]{:S(2)}) copy-start(s32[9]{0:T(128)} %multiply_add_fusion) | copy-start | bytes 112
  539.2 6.9 copy-start.8
  539.2 304.2 %all-to-all-start.3 = ((bf16[16,2,262144]{2,1,0:T(2,128)(2,1)}), bf16[16,2,262144]{2,1,0:T(2,128)(2,1)}, u32[]{:S(2)}, u32[]{:S(2)}) async-start(bf16[16,2,262144]{2,1,0:T(2,128)(2,1)} %reshape.358), calls=%async_computation.3 | async-start | bytes 33554432 | tf_op jit(solution)/shard_map/all_to_all | solution.py:174
Sparse Core Ops, SparseCore 0:
  10.7 70.7 all-gather.1
where the time goes:
time: 986 us; the launch traced here: 977 us
  waiting for transfers between devices  381 us (39%)
  matrix products  194 us (20%)
  local copies, waits for them, and re-layouts  161 us (16%)
  other arithmetic  106 us (11%)
  blocking collectives  94.9 us (10%)
  starting transfers between devices  25.1 us (3%)
  between operations  14.6 us (1%)
    all_to_all x1, waiting for transfers between devices, local(): lax.all_to_all(partials.reshape(n_row, cap_row, flat_width), 'row', split...  288 us
    unnamed x1, blocking collectives  94.9 us
    dot_general x6, matrix products, pair_grads(): lax.dot_general(gradient_rows, block_value_rows, forward, preferred_eleme...  62.7 us
    all_gather x1, waiting for transfers between devices, local(): lax.all_gather(local_kv, 'row', axis=0, tiled=True)  52.8 us
    convert_element_type x6, other arithmetic, pair_grads(): (weights * (grad_weights - row_delta) * factor).astype(jnp.bfloat16)  39.9 us
    all_to_all x1, waiting for transfers between devices, local(): lax.all_to_all(outgoing.reshape(n_col, blk_dev, flat_width), 'col', split...  37.2 us
    while x24, local copies, waits for them, and re-layouts  29.6 us
    all_to_all x1, other arithmetic, local(): lax.all_to_all(outgoing.reshape(n_col, blk_dev, flat_width), 'col', split...  26.5 us
  transfers between devices with their start and end apart: 5, of which 4 were waited for; matrix products, arithmetic and copies ran while one was open for 5% of the time, Pallas kernels for 0%

commit v1 on v0

--- a/solution.py
+++ b/solution.py
@@ -10,6 +10,22 @@
 TILE_QUERY_ROWS = 128
 BLOCK_KEY_ROWS = 512
 PICKED_BLOCKS = 3
+
+
+def swapped_with_each(x, axis, split, join):
+    ways, here = (lax.axis_size(axis), lax.axis_index(axis))
+    width = x.shape[split] // ways
+    lengths = list(x.shape)
+    lengths[split] = width
+    height = lengths[join]
+    lengths[join] = height * ways
+    full = jnp.zeros(lengths, x.dtype)
+    for mask in range(ways):
+        part = lax.dynamic_slice_in_dim(x, (here ^ mask) * width, width, axis=split)
+        if mask:
+            part = lax.ppermute(part, axis, [(d, d ^ mask) for d in range(ways)])
+        full = lax.dynamic_update_slice_in_dim(full, part, (here ^ mask) * height, axis=join)
+    return full
 
 
 def sent_to_all(value, axis):
@@ -95,9 +111,7 @@
     picker = (row_ranks[:, None, :] == slot_ids[None, :, None]) & (row_wants[:, None, :] == 1)
     picker = picker.astype(jnp.bfloat16).reshape(n_col * blk_dev, band_rows)
     outgoing = jnp.dot(picker, column, preferred_element_type=jnp.float32).astype(jnp.bfloat16)
-    landed_parts = lax.all_to_all(
-        outgoing.reshape(n_col, blk_dev, flat_width), "col", split_axis=0, concat_axis=0, tiled=True
-    )
+    landed_parts = swapped_with_each(outgoing.reshape(n_col, blk_dev, flat_width), "col", 0, 0)
     landed_parts = landed_parts.reshape(n_col * blk_dev, BLOCK_KEY_ROWS, 2 * kv_width)
     my_lists = tile_block_table.reshape(device_tile_count * PICKED_BLOCKS)
     holder = my_lists // blk_dev

time: 986 us -> 1110 us (1.13)
  local copies, waits for them, and re-layouts: 161 us -> 304 us
  other arithmetic: 106 us -> 73.2 us
  waiting for transfers between devices: 381 us -> 360 us
  starting transfers between devices: 25.1 us -> 38.5 us
    dynamic_update_slice x0 -> x8, local copies, waits for them, and re-layouts: none -> 156 us  [swapped_with_each(): lax.dynamic_update_slice_in_dim(full, part, (here ^ mask) * height, axis=...]
    all_to_all x1 -> x0, waiting for transfers between devices: 37.2 us -> none  [local(): lax.all_to_all(outgoing.reshape(n_col, blk_dev, flat_width), 'col', split...]
    all_to_all x1 -> x0, other arithmetic: 26.5 us -> none  [local(): lax.all_to_all(outgoing.reshape(n_col, blk_dev, flat_width), 'col', split...]
    ppermute x0 -> x7, starting transfers between devices: none -> 19.2 us  [swapped_with_each(): part = lax.ppermute(part, axis, [(d, d ^ mask) for d in range(ways)])]
    ppermute x0 -> x7, waiting for transfers between devices: none -> 19.2 us  [swapped_with_each(): part = lax.ppermute(part, axis, [(d, d ^ mask) for d in range(ways)])]
    unnamed x24, local copies, waits for them, and re-layouts: 25.5 us -> 10.8 us
    while x24, local copies, waits for them, and re-layouts: 29.6 us -> 16.4 us
  transfers between devices with their start and end apart: 5 -> 11, of which waited for: 4 -> 3; matrix products, arithmetic and copies ran while one was open for 5% -> 17% of each run, Pallas kernels for 0% -> 0%
where the time goes in v1:
time: 1110 us; the launch traced here: 1090 us
  waiting for transfers between devices  360 us (32%)
  local copies, waits for them, and re-layouts  304 us (27%)
  matrix products  203 us (18%)
  blocking collectives  97.8 us (9%)
  other arithmetic  73.2 us (7%)
  starting transfers between devices  38.5 us (3%)
  between operations  14.8 us (1%)
    all_to_all x1, waiting for transfers between devices, local(): lax.all_to_all(partials.reshape(n_row, cap_row, flat_width), 'row', split...  298 us
    dynamic_update_slice x8, local copies, waits for them, and re-layouts, swapped_with_each(): lax.dynamic_update_slice_in_dim(full, part, (here ^ mask) * height, axis=...  156 us
    unnamed x1, blocking collectives  97.8 us
    dot_general x6, matrix products, pair_grads(): lax.dot_general(gradient_rows, block_value_rows, forward, preferred_eleme...  72.1 us
    all_gather x1, waiting for transfers between devices, local(): lax.all_gather(local_kv, 'row', axis=0, tiled=True)  42.9 us
    convert_element_type x6, other arithmetic, pair_grads(): (weights * (grad_weights - row_delta) * factor).astype(jnp.bfloat16)  40 us
    dot_general x6, matrix products, pair_grads(): lax.dot_general(weights.astype(jnp.bfloat16), gradient_rows, backward, pr...  24.1 us
    dot_general x1, matrix products, local(): jnp.dot(assign, paired_terms, precision=lax.Precision.HIGHEST, preferred_...  23 us
  transfers between devices with their start and end apart: 11, of which 3 were waited for; matrix products, arithmetic and copies ran while one was open for 17% of the time, Pallas kernels for 0%

profile of v1, /device:TPU:87, one launch (start us, length us, event | category | flops | bytes accessed | tf_op | source)
XLA Modules:
  0.0 1092.6 jit_solution(6598467939229086289)
XLA Ops:
  10.4 5.1 all-to-all-start
  27.6 7.3 all-to-all-start.1
  37.8 42.9 %all-gather.2.cloned.1.call-done = bf16[8192,512]{1,0:T(8,128)(2,1)} async-done(((bf16[512,512]{1,0:T(8,128)(2,1)}), bf16[8192,512]{1,0:T(8,128)(2,1)}) %all-gather.2.cloned.1.call-update) | async-done | bytes 8388624 | tf_op jit(solution)/shard_map/all_gather | solution.py:107
  80.6 7.9 reshape.356
  88.6 4.6 convolution_convert_fusion.1
  93.2 9.9 dynamic-slice_bitcast_fusion.5
  109.8 19.2 %collective-permute-done.1 = bf16[1,1,262144]{2,0,1:T(2,128)(2,1)} collective-permute-done((bf16[1,1,262144]{2,0,1:T(2,128)(2,1)}, bf16[1,1,262144]{2,0,1:T(2,128)(2,1)}, u32[]{:S(2)}, u32[]{:S(2)}) %collective-permute-start.1) | collective-permute-done | bytes 524320 | tf_op jit(solution)/shard_map/ppermute | solution.py:26
  128.9 13.0 %collective-permute-start.6 = (bf16[1,1,262144]{2,0,1:T(2,128)(2,1)S(1)}, bf16[1,1,262144]{2,0,1:T(2,128)(2,1)}, u32[]{:S(2)}, u32[]{:S(2)}) collective-permute-start(bf16[1,1,262144]{2,0,1:T(2,128)(2,1)S(1)} %get-tuple-element.80), channel_id=1, source_target_pairs={{0,7},{1,6},{2,5},{3,4},{4,3},{5,2},{6,1},{7,0},{8,15},{9,14},{10,... | collective-permute-start | bytes 1572872 | tf_op jit(solution)/shard_map/ppermute | solution.py:26
  146.2 19.5 %dynamic_update_slice.35 = bf16[8,1,262144]{2,0,1:T(8,128)(2,1)} dynamic-update-slice(bf16[8,1,262144]{2,0,1:T(8,128)(2,1)} %broadcast_in_dim.72, bf16[1,1,262144]{2,0,1:T(2,128)(2,1)S(1)} %get-tuple-element.87, s32[]{:T(128)S(6)} %select_n.168, s32[]{:T(128)} %constant.136.clone.1, s32[]{:T(128)} %constant.136.clone.1) | dynamic-update-slice | bytes 1048580 | tf_op jit(solution)/shard_map/dynamic_update_slice | solution.py:27
  165.7 19.6 %dynamic_update_slice.36 = bf16[8,1,262144]{2,0,1:T(8,128)(2,1)} dynamic-update-slice(bf16[8,1,262144]{2,0,1:T(8,128)(2,1)} %dynamic_update_slice.35, bf16[1,1,262144]{2,0,1:T(2,128)(2,1)} %collective-permute-done, s32[]{:T(128)S(6)} %select_n.174, s32[]{:T(128)} %constant.136.clone.1, s32[]{:T(128)} %constant.136.clone.1) | dynamic-update-slice | bytes 1048580 | tf_op jit(solution)/shard_map/dynamic_update_slice | solution.py:27
  185.2 19.6 %dynamic_update_slice.37 = bf16[8,1,262144]{2,0,1:T(8,128)(2,1)} dynamic-update-slice(bf16[8,1,262144]{2,0,1:T(8,128)(2,1)} %dynamic_update_slice.36, bf16[1,1,262144]{2,0,1:T(2,128)(2,1)} %collective-permute-done.1, s32[]{:T(128)S(6)} %select_n.175, s32[]{:T(128)} %constant.136.clone.1, s32[]{:T(128)} %constant.136.clone.1) | dynamic-update-slice | bytes 1048580 | tf_op jit(solution)/shard_map/dynamic_update_slice | solution.py:27
  204.8 19.6 %dynamic_update_slice.38 = bf16[8,1,262144]{2,0,1:T(8,128)(2,1)} dynamic-update-slice(bf16[8,1,262144]{2,0,1:T(8,128)(2,1)} %dynamic_update_slice.37, bf16[1,1,262144]{2,0,1:T(2,128)(2,1)} %collective-permute-done.2, s32[]{:T(128)S(6)} %select_n.176, s32[]{:T(128)} %constant.136.clone.1, s32[]{:T(128)} %constant.136.clone.1) | dynamic-update-slice | bytes 1048580 | tf_op jit(solution)/shard_map/dynamic_update_slice | solution.py:27
  224.4 19.6 %dynamic_update_slice.39 = bf16[8,1,262144]{2,0,1:T(8,128)(2,1)} dynamic-update-slice(bf16[8,1,262144]{2,0,1:T(8,128)(2,1)} %dynamic_update_slice.38, bf16[1,1,262144]{2,0,1:T(2,128)(2,1)} %collective-permute-done.3, s32[]{:T(128)S(6)} %select_n.177, s32[]{:T(128)} %constant.136.clone.1, s32[]{:T(128)} %constant.136.clone.1) | dynamic-update-slice | bytes 1048580 | tf_op jit(solution)/shard_map/dynamic_update_slice | solution.py:27
  244.0 19.6 %dynamic_update_slice.40 = bf16[8,1,262144]{2,0,1:T(8,128)(2,1)} dynamic-update-slice(bf16[8,1,262144]{2,0,1:T(8,128)(2,1)} %dynamic_update_slice.39, bf16[1,1,262144]{2,0,1:T(2,128)(2,1)} %collective-permute-done.4, s32[]{:T(128)S(6)} %select_n.178, s32[]{:T(128)} %constant.136.clone.1, s32[]{:T(128)} %constant.136.clone.1) | dynamic-update-slice | bytes 1048580 | tf_op jit(solution)/shard_map/dynamic_update_slice | solution.py:27
  263.5 19.6 %dynamic_update_slice.41 = bf16[8,1,262144]{2,0,1:T(8,128)(2,1)} dynamic-update-slice(bf16[8,1,262144]{2,0,1:T(8,128)(2,1)} %dynamic_update_slice.40, bf16[1,1,262144]{2,0,1:T(2,128)(2,1)} %collective-permute-done.5, s32[]{:T(128)S(6)} %select_n.179, s32[]{:T(128)} %constant.136.clone.1, s32[]{:T(128)} %constant.136.clone.1) | dynamic-update-slice | bytes 1048580 | tf_op jit(solution)/shard_map/dynamic_update_slice | solution.py:27
  283.1 19.6 %dynamic_update_slice.42 = bf16[8,1,262144]{2,0,1:T(8,128)(2,1)} dynamic-update-slice(bf16[8,1,262144]{2,0,1:T(8,128)(2,1)} %dynamic_update_slice.41, bf16[1,1,262144]{2,0,1:T(2,128)(2,1)} %collective-permute-done.6, s32[]{:T(128)S(6)} %select_n.180, s32[]{:T(128)} %constant.136.clone.1, s32[]{:T(128)} %constant.136.clone.1) | dynamic-update-slice | bytes 1048580 | tf_op jit(solution)/shard_map/dynamic_update_slice | solution.py:27
  302.7 5.6 copy.95
  308.3 5.8 gather_fusion.1
  314.1 7.8 gather.20
  321.8 11.5 %fusion.28 = bf16[3,2,2,1536,128]{4,1,2,3,0:T(2,128)(2,1)S(1)} fusion(bf16[3,1536,2,2,128]{4,3,2,1,0:T(2,128)(2,1)} %gather.20, pred[3,1536]{1,0:T(4,128)(4,1)S(1)} %bitcast.169), kind=kLoop, calls=%fused_computation.41 | loop fusion | flops 2359296 | bytes 9441792 | tf_op jit(solution)/shard_map/transpose | solution.py:137
  336.3 226.0 %while.14 = (s32[]{:T(128)}, bf16[6,2048,128]{2,1,0:T(8,128)(2,1)S(1)}, f32[6,1536,128]{2,1,0:T(8,128)}, f32[6,1536,128]{2,1,0:T(8,128)}, s32[6,1536]{1,0:T(8,12...) while((s32[]{:T(128)}, ...), condition=%wide.region_6.7_spmd, body=%wide.region_2.6_spmd.sunk | while | flops 4086294528 | bytes 213654736 | solution.py:157
  348.4 12.0 %multiply_reduce_fusion.2 = (f32[2048]{0:T(1024)S(1)}, f32[2048,1536]{0,1:T(8,128)}) fusion(f32[2048]{0:T(1024)S(1)} %fusion.72, f32[2048,1536]{0,1:T(8,128)} %copy-done, f32[2048]{0:T(1024)S(1)} %get-tuple-element.150, bf16[6,2,1536,128]{3,2,1,0:T(8,128)(2,1)} %get-tuple-element.184, s32[]{:T(128)} %get-tuple-element.165, s32[]{:T(128)S(6)} %add.320, ...), kind=kOutput, calls=%fused_computation.4.clone.1 | convolution fusion | flops 817887232 | bytes 26108932 | tf_op jit(solution)/shard_map/while/body/eval_jaxpr/dot_general | solution.py:61
  360.4 6.7 multiply_convert_fusion.2
  382.0 4.0 fusion.75
  386.0 12.0 %multiply_reduce_fusion.2 = (f32[2048]{0:T(1024)S(1)}, f32[2048,1536]{0,1:T(8,128)}) fusion(f32[2048]{0:T(1024)S(1)} %fusion.72, f32[2048,1536]{0,1:T(8,128)} %copy-done, f32[2048]{0:T(1024)S(1)} %get-tuple-element.150, bf16[6,2,1536,128]{3,2,1,0:T(8,128)(2,1)} %get-tuple-element.184, s32[]{:T(128)} %get-tuple-element.165, s32[]{:T(128)S(6)} %add.320, ...), kind=kOutput, calls=%fused_computation.4.clone.1 | convolution fusion | flops 817887232 | bytes 26108932 | tf_op jit(solution)/shard_map/while/body/eval_jaxpr/dot_general | solution.py:61
  398.0 6.7 multiply_convert_fusion.2
  419.6 4.0 fusion.75
  423.6 12.0 %multiply_reduce_fusion.2 = (f32[2048]{0:T(1024)S(1)}, f32[2048,1536]{0,1:T(8,128)}) fusion(f32[2048]{0:T(1024)S(1)} %fusion.72, f32[2048,1536]{0,1:T(8,128)} %copy-done, f32[2048]{0:T(1024)S(1)} %get-tuple-element.150, bf16[6,2,1536,128]{3,2,1,0:T(8,128)(2,1)} %get-tuple-element.184, s32[]{:T(128)} %get-tuple-element.165, s32[]{:T(128)S(6)} %add.320, ...), kind=kOutput, calls=%fused_computation.4.clone.1 | convolution fusion | flops 817887232 | bytes 26108932 | tf_op jit(solution)/shard_map/while/body/eval_jaxpr/dot_general | solution.py:61
  435.6 6.7 multiply_convert_fusion.2
  461.2 12.0 %multiply_reduce_fusion.2 = (f32[2048]{0:T(1024)S(1)}, f32[2048,1536]{0,1:T(8,128)}) fusion(f32[2048]{0:T(1024)S(1)} %fusion.72, f32[2048,1536]{0,1:T(8,128)} %copy-done, f32[2048]{0:T(1024)S(1)} %get-tuple-element.150, bf16[6,2,1536,128]{3,2,1,0:T(8,128)(2,1)} %get-tuple-element.184, s32[]{:T(128)} %get-tuple-element.165, s32[]{:T(128)S(6)} %add.320, ...), kind=kOutput, calls=%fused_computation.4.clone.1 | convolution fusion | flops 817887232 | bytes 26108932 | tf_op jit(solution)/shard_map/while/body/eval_jaxpr/dot_general | solution.py:61
  473.2 6.7 multiply_convert_fusion.2
  494.8 4.0 fusion.75
  498.8 12.0 %multiply_reduce_fusion.2 = (f32[2048]{0:T(1024)S(1)}, f32[2048,1536]{0,1:T(8,128)}) fusion(f32[2048]{0:T(1024)S(1)} %fusion.72, f32[2048,1536]{0,1:T(8,128)} %copy-done, f32[2048]{0:T(1024)S(1)} %get-tuple-element.150, bf16[6,2,1536,128]{3,2,1,0:T(8,128)(2,1)} %get-tuple-element.184, s32[]{:T(128)} %get-tuple-element.165, s32[]{:T(128)S(6)} %add.320, ...), kind=kOutput, calls=%fused_computation.4.clone.1 | convolution fusion | flops 817887232 | bytes 26108932 | tf_op jit(solution)/shard_map/while/body/eval_jaxpr/dot_general | solution.py:61
  510.8 6.7 multiply_convert_fusion.2
  532.4 4.0 fusion.75
  536.4 12.0 %multiply_reduce_fusion.2 = (f32[2048]{0:T(1024)S(1)}, f32[2048,1536]{0,1:T(8,128)}) fusion(f32[2048]{0:T(1024)S(1)} %fusion.72, f32[2048,1536]{0,1:T(8,128)} %copy-done, f32[2048]{0:T(1024)S(1)} %get-tuple-element.150, bf16[6,2,1536,128]{3,2,1,0:T(8,128)(2,1)} %get-tuple-element.184, s32[]{:T(128)} %get-tuple-element.165, s32[]{:T(128)S(6)} %add.320, ...), kind=kOutput, calls=%fused_computation.4.clone.1 | convolution fusion | flops 817887232 | bytes 26108932 | tf_op jit(solution)/shard_map/while/body/eval_jaxpr/dot_general | solution.py:61
  548.4 6.7 multiply_convert_fusion.2
  562.4 7.1 copy.77
  569.5 6.0 copy.78
  575.5 5.5 maximum_bitcast_fusion
  581.0 22.1 %reshape.362 = f32[9,262144]{1,0:T(8,128)} reshape(f32[3,3,512,2,2,128]{5,4,3,2,1,0:T(2,128)} %maximum_bitcast_fusion) | data formatting | bytes 18874368 | tf_op jit(solution)/shard_map/reshape | solution.py:169
  603.1 23.0 %convolution_convert_fusion = bf16[32,262144]{1,0:T(8,128)(2,1)} fusion(f32[9,262144]{1,0:T(8,128)} %reshape.362, s32[9]{0:T(128)S(1)} %copy-done.8), kind=kOutput, calls=%fused_computation.35 | convolution fusion | flops 914358528 | bytes 26214436 | tf_op jit(solution)/shard_map/dot_general | solution.py:185
  626.1 16.2 %reshape.363 = bf16[16,2,262144]{2,1,0:T(2,128)(2,1)} reshape(bf16[32,262144]{1,0:T(8,128)(2,1)} %convolution_convert_fusion) | data formatting | bytes 33554432 | tf_op jit(solution)/shard_map/reshape | solution.py:189
  642.3 6.9 all-to-all-start.2
  658.5 297.7 %all-to-all-done.2 = bf16[16,2,262144]{2,1,0:T(2,128)(2,1)} async-done(((bf16[16,2,262144]{2,1,0:T(2,128)(2,1)}), bf16[16,2,262144]{2,1,0:T(2,128)(2,1)}, u32[]{:S(2)}, u32[]{:S(2)}) %all-to-all-start.2) | async-done | bytes 16777248 | tf_op jit(solution)/shard_map/all_to_all | solution.py:188
  956.1 18.1 %convolution_bitcast_fusion.2 = f32[8,262144]{1,0:T(8,128)} fusion(bf16[16,2,262144]{2,1,0:T(2,128)(2,1)} %all-to-all-done.2, s32[16,8]{0,1:T(8,128)S(1)} %dynamic-slice_bitcast_fusion.13, pred[16,8]{0,1:T(8,128)(4,1)S(1)} %fusion.40), kind=kOutput, calls=%fused_computation.36 | convolution fusion | flops 134218240 | bytes 25166464 | tf_op jit(solution)/shard_map/dot_general | solution.py:200
  974.3 97.8 %all-reduce.2 = bf16[8,262144]{1,0:T(8,128)(2,1)} all-reduce(f32[8,262144]{1,0:T(8,128)} %convolution_bitcast_fusion.2), channel_id=2, replica_groups=mesh['row'=16,'col'=8] {'col'}, use_global_device_ids=true, to_apply=%region_9.10.clone | all-reduce | flops 2097152 | bytes 12582912
  1072.1 12.1 %fusion.29 = bf16[262144]{0:T(1024)(128)(2,1)S(1)} fusion(bf16[8,262144]{1,0:T(8,128)(2,1)} %all-reduce.2, u32[]{:T(128)} %bitcast.42), kind=kLoop, calls=%fused_computation.45 | loop fusion | bytes 1048580 | tf_op jit(solution)/shard_map/convert.3
  (159 shorter events, 139.4 us)
Async XLA Ops:
  7.2 73.5 %all-gather.2.cloned.1.call-start = ((), (), s32[]{:S(2)}) async-start(), calls=%async_computation.3 | async-start | bytes 8912896 | tf_op jit(solution)/shard_map/all_gather | solution.py:107
  10.4 16.5 %all-to-all-start = ((s32[8,3,3]{2,1,0:T(4,128)}), s32[8,3,3]{2,1,0:T(4,128)S(1)}, u32[]{:S(2)}, u32[]{:S(2)}) async-start(s32[8,3,3]{2,1,0:T(4,128)} %broadcast_in_dim.68), calls=%async_computation | async-start | bytes 32768 | tf_op jit(solution)/shard_map/all_to_all | solution.py:33
  17.1 5.8 copy-start.2
  22.9 3.8 copy-start.7
  27.6 77.0 %all-to-all-start.1 = ((s32[16,3,3]{2,1,0:T(4,128)}), s32[16,3,3]{2,1,0:T(4,128)S(1)}, u32[]{:S(2)}, u32[]{:S(2)}) async-start(s32[16,3,3]{2,1,0:T(4,128)} %broadcast_in_dim.74), calls=%async_computation.1 | async-start | bytes 65536 | tf_op jit(solution)/shard_map/all_to_all | solution.py:33
  103.1 6.4 collective-permute-start
  103.9 25.0 %collective-permute-start.1 = (bf16[1,1,262144]{2,0,1:T(2,128)(2,1)}, bf16[1,1,262144]{2,0,1:T(2,128)(2,1)}, u32[]{:S(2)}, u32[]{:S(2)}) collective-permute-start(bf16[1,1,262144]{2,0,1:T(2,128)(2,1)} %get-tuple-element.85), channel_id=1, source_target_pairs={{0,2},{1,3},{2,0},{3,1},{4,6},{5,7},{6,4},{7,5},{8,10},{9,11},{10,... | collective-permute-start | bytes 1572872 | tf_op jit(solution)/shard_map/ppermute | solution.py:26
  104.9 119.4 %copy-start.5 = (s32[16,128]{0,1:T(8,128)}, s32[16,128]{0,1:T(8,128)S(1)}, u32[]{:S(2)}) copy-start(s32[16,128]{0,1:T(8,128)S(1)} %copy.75) | copy-start | bytes 24580
  105.0 99.8 %collective-permute-start.2 = (bf16[1,1,262144]{2,0,1:T(2,128)(2,1)}, bf16[1,1,262144]{2,0,1:T(2,128)(2,1)}, u32[]{:S(2)}, u32[]{:S(2)}) collective-permute-start(bf16[1,1,262144]{2,0,1:T(2,128)(2,1)} %get-tuple-element.84), channel_id=1, source_target_pairs={{0,3},{1,2},{2,1},{3,0},{4,7},{5,6},{6,5},{7,4},{8,11},{9,10},{10,... | collective-permute-start | bytes 1572872 | tf_op jit(solution)/shard_map/ppermute | solution.py:26
  106.2 118.2 %collective-permute-start.3 = (bf16[1,1,262144]{2,0,1:T(2,128)(2,1)}, bf16[1,1,262144]{2,0,1:T(2,128)(2,1)}, u32[]{:S(2)}, u32[]{:S(2)}) collective-permute-start(bf16[1,1,262144]{2,0,1:T(2,128)(2,1)} %get-tuple-element.83), channel_id=1, source_target_pairs={{0,4},{1,5},{2,6},{3,7},{4,0},{5,1},{6,2},{7,3},{8,12},{9,13},{10,... | collective-permute-start | bytes 1572872 | tf_op jit(solution)/shard_map/ppermute | solution.py:26
  107.3 136.6 %collective-permute-start.4 = (bf16[1,1,262144]{2,0,1:T(2,128)(2,1)}, bf16[1,1,262144]{2,0,1:T(2,128)(2,1)}, u32[]{:S(2)}, u32[]{:S(2)}) collective-permute-start(bf16[1,1,262144]{2,0,1:T(2,128)(2,1)} %get-tuple-element.82), channel_id=1, source_target_pairs={{0,5},{1,4},{2,7},{3,6},{4,1},{5,0},{6,3},{7,2},{8,13},{9,12},{10,... | collective-permute-start | bytes 1572872 | tf_op jit(solution)/shard_map/ppermute | solution.py:26
  109.5 154.0 %collective-permute-start.5 = (bf16[1,1,262144]{2,0,1:T(2,128)(2,1)S(1)}, bf16[1,1,262144]{2,0,1:T(2,128)(2,1)}, u32[]{:S(2)}, u32[]{:S(2)}) collective-permute-start(bf16[1,1,262144]{2,0,1:T(2,128)(2,1)S(1)} %get-tuple-element.81), channel_id=1, source_target_pairs={{0,6},{1,7},{2,4},{3,5},{4,2},{5,3},{6,0},{7,1},{8,14},{9,15},{10,... | collective-permute-start | bytes 1572872 | tf_op jit(solution)/shard_map/ppermute | solution.py:26
  128.9 154.2 %collective-permute-start.6 = (bf16[1,1,262144]{2,0,1:T(2,128)(2,1)S(1)}, bf16[1,1,262144]{2,0,1:T(2,128)(2,1)}, u32[]{:S(2)}, u32[]{:S(2)}) collective-permute-start(bf16[1,1,262144]{2,0,1:T(2,128)(2,1)S(1)} %get-tuple-element.80), channel_id=1, source_target_pairs={{0,7},{1,6},{2,5},{3,4},{4,3},{5,2},{6,1},{7,0},{8,15},{9,14},{10,... | collective-permute-start | bytes 1572872 | tf_op jit(solution)/shard_map/ppermute | solution.py:26
  142.0 0.6 copy-start.6
  333.4 3.0 copy-start.3
  339.8 4.6 copy-start
  348.4 12.0 %copy-start.1 = (f32[2048,1536]{0,1:T(8,128)S(1)}, f32[2048,1536]{0,1:T(8,128)}, u32[]{:S(2)}) copy-start(f32[2048,1536]{0,1:T(8,128)} %copy-done) | copy-start | bytes 37748740 | tf_op jit(solution)/shard_map/while
  377.4 4.6 copy-start
  386.0 12.0 %copy-start.1 = (f32[2048,1536]{0,1:T(8,128)S(1)}, f32[2048,1536]{0,1:T(8,128)}, u32[]{:S(2)}) copy-start(f32[2048,1536]{0,1:T(8,128)} %copy-done) | copy-start | bytes 37748740 | tf_op jit(solution)/shard_map/while
  415.0 4.6 copy-start
  423.6 12.0 %copy-start.1 = (f32[2048,1536]{0,1:T(8,128)S(1)}, f32[2048,1536]{0,1:T(8,128)}, u32[]{:S(2)}) copy-start(f32[2048,1536]{0,1:T(8,128)} %copy-done) | copy-start | bytes 37748740 | tf_op jit(solution)/shard_map/while
  452.6 4.6 copy-start
  461.2 12.0 %copy-start.1 = (f32[2048,1536]{0,1:T(8,128)S(1)}, f32[2048,1536]{0,1:T(8,128)}, u32[]{:S(2)}) copy-start(f32[2048,1536]{0,1:T(8,128)} %copy-done) | copy-start | bytes 37748740 | tf_op jit(solution)/shard_map/while
  490.2 4.6 copy-start
  498.8 12.0 %copy-start.1 = (f32[2048,1536]{0,1:T(8,128)S(1)}, f32[2048,1536]{0,1:T(8,128)}, u32[]{:S(2)}) copy-start(f32[2048,1536]{0,1:T(8,128)} %copy-done) | copy-start | bytes 37748740 | tf_op jit(solution)/shard_map/while
  527.8 4.6 copy-start
  536.4 12.0 %copy-start.1 = (f32[2048,1536]{0,1:T(8,128)S(1)}, f32[2048,1536]{0,1:T(8,128)}, u32[]{:S(2)}) copy-start(f32[2048,1536]{0,1:T(8,128)} %copy-done) | copy-start | bytes 37748740 | tf_op jit(solution)/shard_map/while
  562.3 13.1 %copy-start.4 = (bf16[6,2048,128]{2,1,0:T(8,128)(2,1)}, bf16[6,2048,128]{2,1,0:T(8,128)(2,1)S(1)}, u32[]{:S(2)}) copy-start(bf16[6,2048,128]{2,1,0:T(8,128)(2,1)S(1)} %get-tuple-element.52) | copy-start | bytes 9437188
  581.0 22.1 %copy-start.8 = (s32[9]{0:T(128)S(1)}, s32[9]{0:T(128)}, u32[]{:S(2)}) copy-start(s32[9]{0:T(128)} %multiply_add_fusion) | copy-start | bytes 112
  642.3 6.9 copy-start.9
  642.3 313.8 %all-to-all-start.2 = ((bf16[16,2,262144]{2,1,0:T(2,128)(2,1)}), bf16[16,2,262144]{2,1,0:T(2,128)(2,1)}, u32[]{:S(2)}, u32[]{:S(2)}) async-start(bf16[16,2,262144]{2,1,0:T(2,128)(2,1)} %reshape.363), calls=%async_computation.2 | async-start | bytes 33554432 | tf_op jit(solution)/shard_map/all_to_all | solution.py:188
Sparse Core Ops, SparseCore 0:
  10.1 70.4 all-gather.1
